TPU v7x, 256 devices: a whole 4x4x8 slice. The times are simulated.
256 devices in a mesh: row: 16 (over x_lo, y, core), col: 16 (over z, x_hi).
Axes of the slice: x: 4 (x_hi: 2, x_lo: 2; x = x_hi * 2 + x_lo), y: 4, z: 8, core: 2. Of those that a mesh axis runs over, the one named last changes fastest.
Arguments:
- labels: int32 [16, 512, 2048], P(None, 'row', 'col'), may hold values from 0 to 11
- pressure: float32 [16, 512, 2048], P(None, 'row', 'col'), may hold values from -6 to 6
- velocity_x: float32 [16, 512, 2048], P(None, 'row', 'col'), may hold values from -6 to 6
- velocity_y: float32 [16, 512, 2048], P(None, 'row', 'col'), may hold values from -6 to 6
- velocity_z: float32 [16, 512, 2048], P(None, 'row', 'col'), may hold values from -6 to 6
- speed_table: float32 [12], replicated, may hold values from 0.8 to 2
- density_table: float32 [12], replicated, may hold values from 0.9 to 1.9
- filter_taps: float32 [33], replicated, may hold values from -0.2 to 0.8, as said below
- layer_width: int32 [4], replicated, may hold values from 10 to 40
Outputs:
- pressure_next: float32 [16, 512, 2048], P(None, 'row', 'col')
- velocity_x_next: float32 [16, 512, 2048], P(None, 'row', 'col')
- velocity_y_next: float32 [16, 512, 2048], P(None, 'row', 'col')
- velocity_z_next: float32 [16, 512, 2048], P(None, 'row', 'col')
Inputs may be any that keep to these rules, and one draw needn't show every extreme that they name: `filter_taps`: tap k weighs the cell k - 16 positions away.
All inputs are finite; a program needn't handle non-finite values.
Results may differ from a plain program's by a relative error of at most 0.000068.
Values sent between devices are 32-bit elements; how exact they have to be, the bound alone decides.
A program may use at most 64 MiB of HBM per device.

v0:
```python
import math
import jax
import jax.numpy as jnp
from jax import lax
from jax.sharding import PartitionSpec as P

time_step = 0.15
reference_speed = 2.0
absorption = 6.0
highest = lax.Precision.HIGHEST


def extended(array, sides, width):
    for axis, dim in sides:
        size, length = (lax.axis_size(axis), array.shape[dim])
        up = [(i, (i + 1) % size) for i in range(size)]
        down = [(j, i) for i, j in up]
        last = lax.slice_in_dim(array, length - width, length, axis=dim)
        initial = lax.slice_in_dim(array, 0, width, axis=dim)
        before = lax.ppermute(last, axis, up)
        after = lax.ppermute(initial, axis, down)
        array = jnp.concatenate([before, array, after], axis=dim)
    return array


def factor_pair(length):
    leading = math.gcd(length, 2 ** ((length.bit_length() - 1) // 2))
    return (leading, length // leading)


def angle_table(height, breadth, length, phase_sign):
    product = (
        jnp.arange(height, dtype=jnp.int32)[:, None]
        * jnp.arange(breadth, dtype=jnp.int32)[None, :]
        % length
    )
    angles = product.astype(jnp.float32) * (2.0 * math.pi / length)
    return (jnp.cos(angles), phase_sign * jnp.sin(angles))


def complex_contract(pieces, tables, form):
    real_part, imag_part = pieces
    cosines, sine_part = tables

    def product(operand, matrix):
        return jnp.einsum(form, operand, matrix, precision=highest)

    return (
        product(real_part, cosines) - product(imag_part, sine_part),
        product(real_part, sine_part) + product(imag_part, cosines),
    )


def complex_times(factor, pieces):
    return (
        factor[0] * pieces[0] - factor[1] * pieces[1],
        factor[0] * pieces[1] + factor[1] * pieces[0],
    )


def line_transform(pieces, on_last, inverse):
    real_part, imag_part = pieces
    position = real_part.ndim - 1 if on_last else real_part.ndim - 2
    length = real_part.shape[position]
    leading, trailing = factor_pair(length)
    phase_sign = 1.0 if inverse else -1.0
    new_shape = real_part.shape[:position] + (leading, trailing) + real_part.shape[position + 1 :]
    pieces = (real_part.reshape(new_shape), imag_part.reshape(new_shape))
    outer_table = angle_table(leading, leading, leading, phase_sign)
    inner_table = angle_table(trailing, trailing, trailing, phase_sign)
    twiddle = angle_table(leading, trailing, length, phase_sign)
    suffix = ""
    if not on_last:
        twiddle = (twiddle[0][:, :, None], twiddle[1][:, :, None])
        suffix = "x"
    if inverse:
        pieces = complex_contract(pieces, inner_table, "...kl" + suffix + ",lb->...kb" + suffix)
        pieces = complex_times(twiddle, pieces)
        pieces = complex_contract(pieces, outer_table, "...kb" + suffix + ",ka->...ab" + suffix)
        factor = 1.0 / length
        pieces = (pieces[0] * factor, pieces[1] * factor)
    else:
        pieces = complex_contract(pieces, outer_table, "...ab" + suffix + ",ak->...kb" + suffix)
        pieces = complex_times(twiddle, pieces)
        pieces = complex_contract(pieces, inner_table, "...kb" + suffix + ",bl->...kl" + suffix)
    initial = real_part.shape
    return (pieces[0].reshape(initial), pieces[1].reshape(initial))


def transform_x(pieces):
    return line_transform(pieces, True, False)


def transform_y(pieces):
    return line_transform(pieces, False, False)


def untransform_x(pieces):
    return line_transform(pieces, True, True)


def untransform_y(pieces):
    return line_transform(pieces, False, True)


def depth_forward(pieces):
    length = pieces[0].shape[1]
    return complex_contract(pieces, angle_table(length, length, length, -1.0), "fzyx,zk->fkyx")


def depth_inverse(pieces):
    length = pieces[0].shape[1]
    result = complex_contract(pieces, angle_table(length, length, length, 1.0), "fkyx,kz->fzyx")
    factor = 1.0 / length
    return (result[0] * factor, result[1] * factor)


def packed(operation, stacked):
    result = operation((stacked[0], stacked[1]))
    return jnp.stack([result[0], result[1]])


def natural_wave(indices, length):
    signed = jnp.where(indices < length // 2, indices, indices - length)
    return signed.astype(jnp.float32) * (2.0 * math.pi / length)


def ordered_wave(position, length):
    leading, trailing = factor_pair(length)
    return natural_wave(position // trailing + leading * (position % trailing), length)


def forward_rows(pieces):
    pieces = depth_forward(pieces)
    stacked = jnp.stack([pieces[0], pieces[1]])
    stacked = packed(
        transform_y, lax.all_to_all(stacked, "row", split_axis=2, concat_axis=3, tiled=True)
    )
    stacked = packed(
        transform_x, lax.all_to_all(stacked, "col", split_axis=3, concat_axis=4, tiled=True)
    )
    return (stacked[0], stacked[1])


def inverse_rows(pieces):
    pieces = untransform_x(pieces)
    stacked = jnp.stack([pieces[0], pieces[1]])
    stacked = packed(
        untransform_y, lax.all_to_all(stacked, "col", split_axis=4, concat_axis=3, tiled=True)
    )
    stacked = packed(
        depth_inverse, lax.all_to_all(stacked, "row", split_axis=3, concat_axis=2, tiled=True)
    )
    return (stacked[0], stacked[1])


def waves_rows(spectral_shape):
    planes, height, breadth = (spectral_shape[1], spectral_shape[2], spectral_shape[3])
    depth_ids = lax.axis_index("row") * planes + jnp.arange(planes, dtype=jnp.int32)
    cross_ids = lax.axis_index("col") * height + jnp.arange(height, dtype=jnp.int32)
    wave_z = natural_wave(depth_ids, planes * lax.axis_size("row"))[:, None, None]
    wave_y = ordered_wave(cross_ids, height * lax.axis_size("col"))[None, :, None]
    wave_x = ordered_wave(jnp.arange(breadth, dtype=jnp.int32), breadth)[None, None, :]
    return (wave_z, wave_y, wave_x)


def derivative(wavenum, correction, phase_sign):
    half_wave = 0.5 * wavenum
    return (
        phase_sign * wavenum * jnp.sin(half_wave) * correction,
        wavenum * jnp.cos(half_wave) * correction,
    )


def band_matrix(filter_taps, extent):
    tap_count = filter_taps.shape[0]
    offset = (
        jnp.arange(extent + tap_count - 1, dtype=jnp.int32)[:, None]
        - jnp.arange(extent, dtype=jnp.int32)[None, :]
    )
    selected = offset[:, :, None] == jnp.arange(tap_count, dtype=jnp.int32)[None, None, :]
    return jnp.sum(jnp.where(selected, filter_taps[None, None, :], 0.0), axis=2)


def absorber(position, length, low_width, high_width):
    low_part = jnp.maximum(low_width - position, 0).astype(jnp.float32) / low_width.astype(
        jnp.float32
    )
    high_part = jnp.maximum(position - (length - 1 - high_width), 0).astype(
        jnp.float32
    ) / high_width.astype(jnp.float32)
    damping = absorption * reference_speed * (low_part**4 + high_part**4)
    return jnp.exp(-0.5 * time_step * damping)


def spectral_correction(wave_z, wave_y, wave_x):
    return jnp.sinc(
        reference_speed
        * time_step
        * jnp.sqrt(wave_x * wave_x + wave_y * wave_y + wave_z * wave_z)
        / (2.0 * math.pi)
    )


def on_device(
    labels,
    pressure,
    velocity_x,
    velocity_y,
    velocity_z,
    speed_table,
    density_table,
    filter_taps,
    layer_width,
):
    planes, height, breadth = pressure.shape
    buoyancy_of = 1.0 / density_table
    modulus_of = density_table * speed_table * speed_table
    buoyancy = jnp.zeros(pressure.shape, jnp.float32)
    modulus = jnp.zeros(pressure.shape, jnp.float32)
    for label_id in range(speed_table.shape[0]):
        matches = labels == label_id
        buoyancy = jnp.where(matches, buoyancy_of[label_id], buoyancy)
        modulus = jnp.where(matches, modulus_of[label_id], modulus)
    coefficients = jnp.stack([buoyancy, modulus])
    reach = filter_taps.shape[0] // 2
    across = band_matrix(filter_taps, breadth)
    downward = band_matrix(filter_taps, height)
    padded = extended(coefficients, (("col", 3),), reach)
    smoothed = jnp.einsum("fzyj,ji->fzyi", padded, across, precision=highest)
    padded = extended(smoothed, (("row", 2),), reach)
    smoothed = jnp.einsum("fzjx,jy->fzyx", padded, downward, precision=highest)
    buoyancy = smoothed[0]
    modulus = smoothed[1]
    column_ids = lax.axis_index("col") * breadth + jnp.arange(breadth, dtype=jnp.int32)
    row_ids = lax.axis_index("row") * height + jnp.arange(height, dtype=jnp.int32)
    damp_x = absorber(column_ids, breadth * lax.axis_size("col"), layer_width[0], layer_width[1])[
        None, None, :
    ]
    damp_y = absorber(row_ids, height * lax.axis_size("row"), layer_width[2], layer_width[3])[
        None, :, None
    ]
    empty = jnp.zeros(pressure.shape, jnp.float32)
    forward, inverse, waves_of = (forward_rows, inverse_rows, waves_rows)
    pressure_hat = forward((pressure[None], empty[None]))
    wave_z, wave_y, wave_x = waves_of(pressure_hat[0].shape)
    correction = spectral_correction(wave_z, wave_y, wave_x)
    pressure_one = (pressure_hat[0][0], pressure_hat[1][0])
    grad_x_hat = complex_times(derivative(wave_x, correction, -1.0), pressure_one)
    grad_y_hat = complex_times(derivative(wave_y, correction, -1.0), pressure_one)
    grad_z_hat = complex_times(derivative(wave_z, correction, -1.0), pressure_one)
    packed_real = jnp.stack([grad_x_hat[0] - grad_y_hat[1], grad_z_hat[0]])
    packed_imag = jnp.stack([grad_x_hat[1] + grad_y_hat[0], grad_z_hat[1]])
    gradients = inverse((packed_real, packed_imag))
    grad_x = gradients[0][0]
    grad_y = gradients[1][0]
    grad_z = gradients[0][1]
    next_x = damp_x * (damp_x * velocity_x - time_step * buoyancy * grad_x)
    next_y = damp_y * (damp_y * velocity_y - time_step * buoyancy * grad_y)
    next_z = velocity_z - time_step * buoyancy * grad_z
    velocity_hat = forward((jnp.stack([next_x, next_z]), jnp.stack([next_y, empty])))
    horizontal = (velocity_hat[0][0], velocity_hat[1][0])
    vertical = (velocity_hat[0][1], velocity_hat[1][1])
    flow_x = complex_times(derivative(wave_x, correction, 1.0), horizontal)
    flow_y = complex_times(derivative(wave_y, correction, 1.0), horizontal)
    flow_z = complex_times(derivative(wave_z, correction, 1.0), vertical)
    summed_real = flow_x[0] + flow_y[1] + flow_z[0]
    summed_imag = flow_x[1] - flow_y[0] + flow_z[1]
    divergence = inverse((summed_real[None], summed_imag[None]))[0][0]
    damp_both = damp_x * damp_y
    pressure_next = damp_both * (damp_both * pressure - time_step * modulus * divergence)
    return (pressure_next, next_x, next_y, next_z)


def solution(mesh):
    return jax.shard_map(
        on_device,
        mesh=mesh,
        in_specs=(
            P(None, "row", "col"),
            P(None, "row", "col"),
            P(None, "row", "col"),
            P(None, "row", "col"),
            P(None, "row", "col"),
            P(),
            P(),
            P(),
            P(),
        ),
        out_specs=(
            P(None, "row", "col"),
            P(None, "row", "col"),
            P(None, "row", "col"),
            P(None, "row", "col"),
        ),
        check_vma=False,
    )
```

profile of v0, /device:TPU:1, one launch (start us, length us, event | category | flops | bytes accessed | tf_op | source)
XLA Modules:
  0.0 320.3 jit_solution(11069281004676494393)
XLA Ops:
  5.2 6.9 %all-to-all-start = ((f32[2,1,16,32,128]{4,3,1,0,2:T(8,128)}), f32[2,1,16,32,128]{4,3,1,0,2:T(8,128)S(1)}, u32[]{:S(2)}, u32[]{:S(2)}) async-start(f32[2,1,16,32,128]{4,3,1,0,2:T(8,128)} %copy.316), calls=%async_computation | async-start | bytes 1048576 | tf_op jit(solution)/shard_map/all_to_all | solution.py:137
  12.4 9.4 %all-to-all-done = f32[2,1,16,32,128]{4,3,1,0,2:T(8,128)S(1)} async-done(((f32[2,1,16,32,128]{4,3,1,0,2:T(8,128)}), f32[2,1,16,32,128]{4,3,1,0,2:T(8,128)S(1)}, u32[]{:S(2)}, u32[]{:S(2)}) %all-to-all-start) | async-done | bytes 524320 | tf_op jit(solution)/shard_map/all_to_all | solution.py:137
  27.1 10.6 %all-to-all-start.1 = ((f32[2,1,1,512,128]{4,2,1,0,3:T(1,128)}), f32[2,1,1,512,128]{4,2,1,0,3:T(1,128)S(1)}, u32[]{:S(2)}, u32[]{:S(2)}) async-start(f32[2,1,1,512,128]{4,2,1,0,3:T(1,128)} %pad_maximum_fusion.6), calls=%async_computation.1 | async-start | bytes 1048576 | tf_op jit(solution)/shard_map/all_to_all | solution.py:140
  39.0 15.4 %all-to-all-done.1 = f32[2,1,1,512,128]{4,2,1,0,3:T(1,128)S(1)} async-done(((f32[2,1,1,512,128]{4,2,1,0,3:T(1,128)}), f32[2,1,1,512,128]{4,2,1,0,3:T(1,128)S(1)}, u32[]{:S(2)}, u32[]{:S(2)}) %all-to-all-start.1) | async-done | bytes 524320 | tf_op jit(solution)/shard_map/all_to_all | solution.py:140
  70.8 3.9 %copy.390 = f32[2,1,32,32,64]{2,0,4,3,1:T(2,128)} copy(f32[2,1,32,32,64]{4,3,2,0,1:T(8,128)} %fusion.5) | data formatting | bytes 1048576 | tf_op jit(solution)/shard_map/stack;reshape | solution.py:147
  76.8 4.1 %copy.391 = f32[2,1,32,32,64]{2,0,4,3,1:T(2,128)} copy(f32[2,1,32,32,64]{4,3,2,0,1:T(8,128)} %fusion.3) | data formatting | bytes 1048576 | tf_op jit(solution)/shard_map/stack;reshape | solution.py:147
  80.9 5.2 %fusion.760 = f32[2048,2,1,2,32]{4,3,2,1,0:T(2,128)} fusion(f32[1,2,1,32,2048]{3,1,2,0,4:T(2,128)} %bitcast.572, f32[1,2,1,32,2048]{3,1,2,0,4:T(2,128)S(1)} %bitcast.571), kind=kLoop, calls=%fused_computation.852 | loop fusion | flops 262144 | bytes 2097152
  86.1 6.6 %reshape.1299 = f32[16,1,16384]{2,1,0:T(1,128)} reshape(f32[2048,2,1,2,32]{4,3,2,1,0:T(2,128)} %fusion.760) | data formatting | bytes 2097152
  92.7 4.5 %all-to-all-start.2 = ((f32[16,1,16384]{2,1,0:T(1,128)}), f32[16,1,16384]{2,1,0:T(1,128)S(1)}, u32[]{:S(2)}, u32[]{:S(2)}) async-start(f32[16,1,16384]{2,1,0:T(1,128)} %reshape.1299), calls=%async_computation.2 | async-start | bytes 2097152 | tf_op jit(solution)/shard_map/all_to_all | solution.py:149
  98.6 8.1 %select_bitcast_fusion.1 = (f32[1,16,32,128]{3,2,1,0:T(8,128)S(1)}, pred[16,32,128]{2,1,0:T(8,128)(4,1)S(1)}, pred[16,32,128]{2,1,0:T(8,128)(4,1)S(1)}, pred[16,...) fusion(f32[]{:T(128)} %bitcast.19, f32[]{:T(128)} %bitcast.18, ...), kind=kLoop, calls=%fused_computation.230 | loop fusion | flops 1572864 | bytes 1310768 | tf_op jit(solution)/shard_map/stack | solution.py:225
  106.7 7.7 %select_bitcast_fusion = f32[1,16,32,128]{3,2,1,0:T(8,128)S(1)} fusion(pred[16,32,128]{2,1,0:T(8,128)(4,1)S(1)} %get-tuple-element.16, pred[16,32,128]{2,1,0:T(8,128)(4,1)S(1)} %get-tuple-element.15, pred[16,32,128]{2,1,0:T(8,128)(4,1)S(1)} %get-tuple-element.14, pred[16,32,128]{2,1,0:T(8,128)(4,1)S(1)} %get-tuple-element.13, ...), kind=kLoop, calls=%fused_computation.229 | loop fusion | flops 786432 | bytes 1048624 | tf_op jit(solution)/shard_map/stack | solution.py:225
  115.4 2.9 collective-permute-start
  127.2 3.1 reduce
  130.4 5.1 %reshape.1300 = f32[2048,2,1,2,32]{4,3,2,1,0:T(2,128)} reshape(f32[16,16384]{1,0:T(8,128)S(1)} %reduce) | data formatting | bytes 2097152
  135.4 5.2 %copy.330 = f32[2,2,1,32,16,128]{5,3,4,1,2,0:T(8,128)S(1)} copy(f32[2,2,1,32,16,128]{3,1,0,5,4,2:T(2,128)} %bitcast.564) | data formatting | bytes 2097152 | tf_op jit(solution)/shard_map/all_to_all | solution.py:149
  149.1 6.5 %all-to-all-start.3 = ((f32[2,2,1,512,128]{4,1,2,0,3:T(2,128)}), f32[2,2,1,512,128]{4,1,2,0,3:T(2,128)S(1)}, u32[]{:S(2)}, u32[]{:S(2)}) async-start(f32[2,2,1,512,128]{4,1,2,0,3:T(2,128)} %copy.337), calls=%async_computation.3 | async-start | bytes 2097152 | tf_op jit(solution)/shard_map/all_to_all | solution.py:152
  155.6 2.3 fusion.28
  161.3 9.6 %collective-permute-done.2 = f32[2,16,16,128]{3,2,1,0:T(8,128)S(1)} collective-permute-done((f32[2,16,16,128]{3,2,1,0:T(8,128)S(1)}, f32[2,16,16,128]{3,2,1,0:T(8,128)S(1)}, u32[]{:S(2)}, u32[]{:S(2)}) %collective-permute-start.2) | collective-permute-done | bytes 262176 | tf_op jit(solution)/shard_map/ppermute | solution.py:20
  181.5 20.8 %all_to_all.96 = f32[2,2,16,32,128]{4,3,1,0,2:T(8,128)S(1)} all-to-all(f32[2,2,16,32,128]{4,3,1,0,2:T(8,128)S(1)} %copy.352), channel_id=1, replica_groups=mesh['row'=16,'col'=16] {'row'}, dimensions={2} | all-to-all | bytes 2097152 | tf_op jit(solution)/shard_map/all_to_all | solution.py:137
  211.3 7.5 %all-to-all-start.5 = ((f32[2,2,1,512,128]{4,1,2,0,3:T(2,128)}), f32[2,2,1,512,128]{4,1,2,0,3:T(2,128)S(1)}, u32[]{:S(2)}, u32[]{:S(2)}) async-start(f32[2,2,1,512,128]{4,1,2,0,3:T(2,128)} %pad_maximum_fusion.3), calls=%async_computation.5 | async-start | bytes 2097152 | tf_op jit(solution)/shard_map/all_to_all | solution.py:140
  218.8 25.9 %all-to-all-done.5 = f32[2,2,1,512,128]{4,1,2,0,3:T(2,128)S(1)} async-done(((f32[2,2,1,512,128]{4,1,2,0,3:T(2,128)}), f32[2,2,1,512,128]{4,1,2,0,3:T(2,128)S(1)}, u32[]{:S(2)}, u32[]{:S(2)}) %all-to-all-start.5) | async-done | bytes 1048608 | tf_op jit(solution)/shard_map/all_to_all | solution.py:140
  267.2 24.5 %all_to_all.97 = f32[16,1,8192]{2,1,0:T(1,128)S(1)} all-to-all(f32[16,1,8192]{2,1,0:T(1,128)S(1)} %reshape.1301), channel_id=1, replica_groups=mesh['row'=16,'col'=16] {'col'}, dimensions={0} | all-to-all | bytes 1048576 | tf_op jit(solution)/shard_map/all_to_all | solution.py:149
  301.7 6.1 %all-to-all-start.7 = ((f32[2,1,1,512,128]{4,2,1,0,3:T(1,128)}), f32[2,1,1,512,128]{4,2,1,0,3:T(1,128)S(1)}, u32[]{:S(2)}, u32[]{:S(2)}) async-start(f32[2,1,1,512,128]{4,2,1,0,3:T(1,128)} %copy.372), calls=%async_computation.7 | async-start | bytes 1048576 | tf_op jit(solution)/shard_map/all_to_all | solution.py:152
  307.9 9.7 %all-to-all-done.7 = f32[2,1,1,512,128]{4,2,1,0,3:T(1,128)S(1)} async-done(((f32[2,1,1,512,128]{4,2,1,0,3:T(1,128)}), f32[2,1,1,512,128]{4,2,1,0,3:T(1,128)S(1)}, u32[]{:S(2)}, u32[]{:S(2)}) %all-to-all-start.7) | async-done | bytes 524320 | tf_op jit(solution)/shard_map/all_to_all | solution.py:152
  (205 shorter events, 102.5 us)
Async XLA Ops:
  5.2 16.6 %all-to-all-start = ((f32[2,1,16,32,128]{4,3,1,0,2:T(8,128)}), f32[2,1,16,32,128]{4,3,1,0,2:T(8,128)S(1)}, u32[]{:S(2)}, u32[]{:S(2)}) async-start(f32[2,1,16,32,128]{4,3,1,0,2:T(8,128)} %copy.316), calls=%async_computation | async-start | bytes 1048576 | tf_op jit(solution)/shard_map/all_to_all | solution.py:137
  27.1 27.3 %all-to-all-start.1 = ((f32[2,1,1,512,128]{4,2,1,0,3:T(1,128)}), f32[2,1,1,512,128]{4,2,1,0,3:T(1,128)S(1)}, u32[]{:S(2)}, u32[]{:S(2)}) async-start(f32[2,1,1,512,128]{4,2,1,0,3:T(1,128)} %pad_maximum_fusion.6), calls=%async_computation.1 | async-start | bytes 1048576 | tf_op jit(solution)/shard_map/all_to_all | solution.py:140
  38.0 21.9 %copy-start.17 = (f32[32]{0:T(128)}, f32[32]{0:T(128)S(1)}, u32[]{:S(2)}) copy-start(f32[32]{0:T(128)S(1)} %get-tuple-element.82) | copy-start | bytes 388
  38.7 21.2 %copy-start.20 = (f32[32]{0:T(128)}, f32[32]{0:T(128)S(1)}, u32[]{:S(2)}) copy-start(f32[32]{0:T(128)S(1)} %get-tuple-element.85) | copy-start | bytes 388
  76.8 4.1 %copy-start = (f32[2,1,32,32,64]{2,0,4,3,1:T(2,128)S(1)}, f32[2,1,32,32,64]{2,0,4,3,1:T(2,128)}, u32[]{:S(2)}) copy-start(f32[2,1,32,32,64]{2,0,4,3,1:T(2,128)} %copy.390) | copy-start | bytes 1572868
  86.1 11.1 %copy-start.22 = (f32[12]{0:T(128)S(1)}, f32[12]{0:T(128)}, u32[]{:S(2)}) copy-start(f32[12]{0:T(128)} %param.14) | copy-start | bytes 148
  86.1 11.1 %copy-start.23 = (f32[12]{0:T(128)S(1)}, f32[12]{0:T(128)}, u32[]{:S(2)}) copy-start(f32[12]{0:T(128)} %param.15) | copy-start | bytes 148
  86.1 12.5 %copy-start.7 = (s32[16,32,128]{2,1,0:T(8,128)S(1)}, s32[16,32,128]{2,1,0:T(8,128)}, u32[]{:S(2)}) copy-start(s32[16,32,128]{2,1,0:T(8,128)} %param.9) | copy-start | bytes 786436
  92.7 27.9 %copy-start.11 = (s32[4]{0:T(128)S(1)}, s32[4]{0:T(128)}, u32[]{:S(2)}) copy-start(s32[4]{0:T(128)} %param.17) | copy-start | bytes 52
  92.7 33.7 %copy-start.16 = (f32[33]{0:T(128)S(1)}, f32[33]{0:T(128)}, u32[]{:S(2)}) copy-start(f32[33]{0:T(128)} %param.16) | copy-start | bytes 400
  92.7 34.0 %all-to-all-start.2 = ((f32[16,1,16384]{2,1,0:T(1,128)}), f32[16,1,16384]{2,1,0:T(1,128)S(1)}, u32[]{:S(2)}, u32[]{:S(2)}) async-start(f32[16,1,16384]{2,1,0:T(1,128)} %reshape.1299), calls=%async_computation.2 | async-start | bytes 2097152 | tf_op jit(solution)/shard_map/all_to_all | solution.py:149
  115.4 40.2 %collective-permute-start = (f32[2,16,32,16]{3,2,1,0:T(8,128)}, f32[2,16,32,16]{3,2,1,0:T(8,128)}, u32[]{:S(2)}, u32[]{:S(2)}) collective-permute-start(f32[2,16,32,16]{3,2,1,0:T(8,128)} %get-tuple-element.48), channel_id=1, source_target_pairs={{0,1},{1,2},{2,3},{3,4},{4,5},{5,6},{6,7},{7,8},{8,9},{9,10},{10,1... | collective-permute-start | bytes 196616 | tf_op jit(solution)/shard_map/ppermute | solution.py:20
  118.3 37.3 %collective-permute-start.1 = (f32[2,16,32,16]{3,2,1,0:T(8,128)S(1)}, f32[2,16,32,16]{3,2,1,0:T(8,128)}, u32[]{:S(2)}, u32[]{:S(2)}) collective-permute-start(f32[2,16,32,16]{3,2,1,0:T(8,128)S(1)} %get-tuple-element.49), channel_id=1, source_target_pairs={{1,0},{2,1},{3,2},{4,3},{5,4},{6,5},{7,6},{8,7},{9,8},{10,9},{11,1... | collective-permute-start | bytes 196616 | tf_op jit(solution)/shard_map/ppermute | solution.py:21
  149.1 24.1 %all-to-all-start.3 = ((f32[2,2,1,512,128]{4,1,2,0,3:T(2,128)}), f32[2,2,1,512,128]{4,1,2,0,3:T(2,128)S(1)}, u32[]{:S(2)}, u32[]{:S(2)}) async-start(f32[2,2,1,512,128]{4,1,2,0,3:T(2,128)} %copy.337), calls=%async_computation.3 | async-start | bytes 2097152 | tf_op jit(solution)/shard_map/all_to_all | solution.py:152
  158.0 12.9 %collective-permute-start.2 = (f32[2,16,16,128]{3,2,1,0:T(8,128)S(1)}, f32[2,16,16,128]{3,2,1,0:T(8,128)S(1)}, u32[]{:S(2)}, u32[]{:S(2)}) collective-permute-start(f32[2,16,16,128]{3,2,1,0:T(8,128)S(1)} %get-tuple-element.46), channel_id=1, source_target_pairs={{0,16},{16,32},{32,48},{48,64},{64,80},{80,96},{96,112},{112,128},... | collective-permute-start | bytes 786440 | tf_op jit(solution)/shard_map/ppermute | solution.py:20
  159.7 12.8 %collective-permute-start.3 = (f32[2,16,16,128]{3,2,1,0:T(8,128)S(1)}, f32[2,16,16,128]{3,2,1,0:T(8,128)S(1)}, u32[]{:S(2)}, u32[]{:S(2)}) collective-permute-start(f32[2,16,16,128]{3,2,1,0:T(8,128)S(1)} %get-tuple-element.47), channel_id=1, source_target_pairs={{16,0},{32,16},{48,32},{64,48},{80,64},{96,80},{112,96},{128,112},... | collective-permute-start | bytes 786440 | tf_op jit(solution)/shard_map/ppermute | solution.py:21
  173.1 4.6 %copy-start.2 = (f32[2,16,32,128]{3,2,1,0:T(8,128)}, f32[2,16,32,128]{3,2,1,0:T(8,128)S(1)}, u32[]{:S(2)}) copy-start(f32[2,16,32,128]{3,2,1,0:T(8,128)S(1)} %convolution_bitcast_fusion) | copy-start | bytes 1572868
  178.1 3.0 copy-start.4
  211.3 33.4 %all-to-all-start.5 = ((f32[2,2,1,512,128]{4,1,2,0,3:T(2,128)}), f32[2,2,1,512,128]{4,1,2,0,3:T(2,128)S(1)}, u32[]{:S(2)}, u32[]{:S(2)}) async-start(f32[2,2,1,512,128]{4,1,2,0,3:T(2,128)} %pad_maximum_fusion.3), calls=%async_computation.5 | async-start | bytes 2097152 | tf_op jit(solution)/shard_map/all_to_all | solution.py:140
  299.1 8.8 %copy-start.13 = (f32[32]{0:T(128)S(1)}, f32[32]{0:T(128)}, u32[]{:S(2)}) copy-start(f32[32]{0:T(128)} %multiply_exponential_fusion) | copy-start | bytes 388
  299.1 8.8 %copy-start.15 = (f32[128]{0:T(128)S(1)}, f32[128]{0:T(128)}, u32[]{:S(2)}) copy-start(f32[128]{0:T(128)} %multiply_exponential_fusion.1) | copy-start | bytes 1540
  300.4 18.7 %copy-start.1 = (f32[16,32,128]{2,1,0:T(8,128)S(1)}, f32[16,32,128]{2,1,0:T(8,128)}, u32[]{:S(2)}) copy-start(f32[16,32,128]{2,1,0:T(8,128)} %param.10) | copy-start | bytes 786436
  300.4 18.7 %copy-start.3 = (f32[2,16,32,128]{3,2,1,0:T(8,128)S(1)}, f32[2,16,32,128]{3,2,1,0:T(8,128)}, u32[]{:S(2)}) copy-start(f32[2,16,32,128]{3,2,1,0:T(8,128)} %copy-done.2) | copy-start | bytes 1572868
  301.7 15.9 %all-to-all-start.7 = ((f32[2,1,1,512,128]{4,2,1,0,3:T(1,128)}), f32[2,1,1,512,128]{4,2,1,0,3:T(1,128)S(1)}, u32[]{:S(2)}, u32[]{:S(2)}) async-start(f32[2,1,1,512,128]{4,2,1,0,3:T(1,128)} %copy.372), calls=%async_computation.7 | async-start | bytes 1048576 | tf_op jit(solution)/shard_map/all_to_all | solution.py:152
  (10 other events, 21.8 us)
where the time goes:
time: 326 us; the launch traced here: 320 us
  waiting for transfers between devices  71.5 us (22%)
  matrix products  66.5 us (20%)
  starting transfers between devices  49.2 us (15%)
  blocking collectives  45.2 us (14%)
  local copies, waits for them, and re-layouts  44 us (13%)
  other arithmetic  37.5 us (12%)
  between operations  6.28 us (2%)
    dot_general x78, matrix products, product(): return jnp.einsum(form, operand, matrix, precision=highest)  63.5 us
    all_to_all x2, waiting for transfers between devices, forward_rows(): lax.all_to_all(stacked, 'col', split_axis=3, concat_axis=4, tiled=True)  41.3 us
    all_to_all x1, blocking collectives, inverse_rows(): lax.all_to_all(stacked, 'col', split_axis=4, concat_axis=3, tiled=True)  24.5 us
    all_to_all x1, blocking collectives, forward_rows(): lax.all_to_all(stacked, 'row', split_axis=2, concat_axis=3, tiled=True)  20.8 us
    all_to_all x2, starting transfers between devices, forward_rows(): lax.all_to_all(stacked, 'col', split_axis=3, concat_axis=4, tiled=True)  18.1 us
    another operation x3, other arithmetic, on_device(): coefficients = jnp.stack([buoyancy, modulus])  16.8 us
    unnamed x55, local copies, waits for them, and re-layouts  15.8 us
    all_to_all x2, starting transfers between devices, inverse_rows(): lax.all_to_all(stacked, 'row', split_axis=3, concat_axis=2, tiled=True)  12.6 us
  transfers between devices with their start and end apart: 10, of which 6 were waited for; matrix products, arithmetic and copies ran while one was open for 15% of the time, Pallas kernels for 0%

commit v1 on v0

--- a/solution.py
+++ b/solution.py
@@ -8,6 +8,12 @@
 reference_speed = 2.0
 absorption = 6.0
 highest = lax.Precision.HIGHEST
+
+
+def exchange_blocks(array, axis, split, join):
+    pieces = jnp.split(array, lax.axis_size(axis), axis=split)
+    incoming = lax.all_to_all(jnp.stack(pieces), axis, 0, 0)
+    return jnp.concatenate(incoming, axis=join)
 
 
 def extended(array, sides, width):
@@ -148,9 +154,7 @@
     stacked = packed(
         untransform_y, lax.all_to_all(stacked, "col", split_axis=4, concat_axis=3, tiled=True)
     )
-    stacked = packed(
-        depth_inverse, lax.all_to_all(stacked, "row", split_axis=3, concat_axis=2, tiled=True)
-    )
+    stacked = packed(depth_inverse, exchange_blocks(stacked, "row", 3, 2))
     return (stacked[0], stacked[1])
 
 

time: 326 us -> 342 us (1.049)
  local copies, waits for them, and re-layouts: 44 us -> 59.4 us
    unnamed x55 -> x83, local copies, waits for them, and re-layouts: 15.8 us -> 34 us
  transfers between devices with their start and end apart: 10 -> 10, of which waited for: 6 -> 6; matrix products, arithmetic and copies ran while one was open for 15% -> 17% of each run, Pallas kernels for 0% -> 0%
where the time goes in v1:
time: 342 us; the launch traced here: 336 us
  waiting for transfers between devices  71.4 us (21%)
  matrix products  65 us (19%)
  local copies, waits for them, and re-layouts  59.4 us (17%)
  starting transfers between devices  49.8 us (15%)
  blocking collectives  45 us (13%)
  other arithmetic  38.7 us (11%)
  between operations  6.24 us (2%)
    dot_general x78, matrix products, product(): return jnp.einsum(form, operand, matrix, precision=highest)  62.1 us
    all_to_all x2, waiting for transfers between devices, forward_rows(): lax.all_to_all(stacked, 'col', split_axis=3, concat_axis=4, tiled=True)  41.1 us
    unnamed x83, local copies, waits for them, and re-layouts  34 us
    all_to_all x1, blocking collectives, inverse_rows(): lax.all_to_all(stacked, 'col', split_axis=4, concat_axis=3, tiled=True)  24.4 us
    all_to_all x1, blocking collectives, forward_rows(): lax.all_to_all(stacked, 'row', split_axis=2, concat_axis=3, tiled=True)  20.6 us
    all_to_all x2, starting transfers between devices, forward_rows(): lax.all_to_all(stacked, 'col', split_axis=3, concat_axis=4, tiled=True)  18.4 us
    another operation x3, other arithmetic, on_device(): coefficients = jnp.stack([buoyancy, modulus])  16.9 us
    all_to_all x2, starting transfers between devices, exchange_blocks(): incoming = lax.all_to_all(jnp.stack(pieces), axis, 0, 0)  12.8 us
  transfers between devices with their start and end apart: 10, of which 6 were waited for; matrix products, arithmetic and copies ran while one was open for 17% of the time, Pallas kernels for 0%

profile of v1, /device:TPU:1, one launch (start us, length us, event | category | flops | bytes accessed | tf_op | source)
XLA Modules:
  0.0 335.6 jit_solution(6054014276593848841)
XLA Ops:
  5.2 6.9 %all-to-all-start = ((f32[2,1,16,32,128]{4,3,1,0,2:T(8,128)}), f32[2,1,16,32,128]{4,3,1,0,2:T(8,128)S(1)}, u32[]{:S(2)}, u32[]{:S(2)}) async-start(f32[2,1,16,32,128]{4,3,1,0,2:T(8,128)} %copy.440), calls=%async_computation | async-start | bytes 1048576 | tf_op jit(solution)/shard_map/all_to_all | solution.py:143
  12.4 9.4 %all-to-all-done = f32[2,1,16,32,128]{4,3,1,0,2:T(8,128)S(1)} async-done(((f32[2,1,16,32,128]{4,3,1,0,2:T(8,128)}), f32[2,1,16,32,128]{4,3,1,0,2:T(8,128)S(1)}, u32[]{:S(2)}, u32[]{:S(2)}) %all-to-all-start) | async-done | bytes 524320 | tf_op jit(solution)/shard_map/all_to_all | solution.py:143
  27.2 10.6 %all-to-all-start.1 = ((f32[2,1,1,512,128]{4,2,1,0,3:T(1,128)}), f32[2,1,1,512,128]{4,2,1,0,3:T(1,128)S(1)}, u32[]{:S(2)}, u32[]{:S(2)}) async-start(f32[2,1,1,512,128]{4,2,1,0,3:T(1,128)} %pad_maximum_fusion.7), calls=%async_computation.1 | async-start | bytes 1048576 | tf_op jit(solution)/shard_map/all_to_all | solution.py:146
  39.0 15.5 %all-to-all-done.1 = f32[2,1,1,512,128]{4,2,1,0,3:T(1,128)S(1)} async-done(((f32[2,1,1,512,128]{4,2,1,0,3:T(1,128)}), f32[2,1,1,512,128]{4,2,1,0,3:T(1,128)S(1)}, u32[]{:S(2)}, u32[]{:S(2)}) %all-to-all-start.1) | async-done | bytes 524320 | tf_op jit(solution)/shard_map/all_to_all | solution.py:146
  70.6 3.9 %copy.536 = f32[2,1,32,32,64]{2,0,4,3,1:T(2,128)} copy(f32[2,1,32,32,64]{4,3,2,0,1:T(8,128)} %fusion.5) | data formatting | bytes 1048576 | tf_op jit(solution)/shard_map/stack;reshape | solution.py:153
  76.6 4.1 %copy.537 = f32[2,1,32,32,64]{2,0,4,3,1:T(2,128)} copy(f32[2,1,32,32,64]{4,3,2,0,1:T(8,128)} %fusion.3) | data formatting | bytes 1048576 | tf_op jit(solution)/shard_map/stack;reshape | solution.py:153
  80.7 5.2 %fusion.756 = f32[2048,2,1,2,32]{4,3,2,1,0:T(2,128)} fusion(f32[1,2,1,32,2048]{3,1,2,0,4:T(2,128)} %bitcast.746, f32[1,2,1,32,2048]{3,1,2,0,4:T(2,128)S(1)} %bitcast.745), kind=kLoop, calls=%fused_computation.920 | loop fusion | flops 262144 | bytes 2097152
  85.9 6.6 %reshape.1299 = f32[16,1,16384]{2,1,0:T(1,128)} reshape(f32[2048,2,1,2,32]{4,3,2,1,0:T(2,128)} %fusion.756) | data formatting | bytes 2097152
  92.5 4.5 %all-to-all-start.2 = ((f32[16,1,16384]{2,1,0:T(1,128)}), f32[16,1,16384]{2,1,0:T(1,128)S(1)}, u32[]{:S(2)}, u32[]{:S(2)}) async-start(f32[16,1,16384]{2,1,0:T(1,128)} %reshape.1299), calls=%async_computation.2 | async-start | bytes 2097152 | tf_op jit(solution)/shard_map/all_to_all | solution.py:155
  98.4 8.1 %select_bitcast_fusion.1 = (f32[1,16,32,128]{3,2,1,0:T(8,128)S(1)}, pred[16,32,128]{2,1,0:T(8,128)(4,1)S(1)}, pred[16,32,128]{2,1,0:T(8,128)(4,1)S(1)}, pred[16,...) fusion(f32[]{:T(128)} %bitcast.19, f32[]{:T(128)} %bitcast.18, ...), kind=kLoop, calls=%fused_computation.236 | loop fusion | flops 1572864 | bytes 1310768 | tf_op jit(solution)/shard_map/stack | solution.py:229
  106.5 7.8 %select_bitcast_fusion = f32[1,16,32,128]{3,2,1,0:T(8,128)S(1)} fusion(pred[16,32,128]{2,1,0:T(8,128)(4,1)S(1)} %get-tuple-element.16, pred[16,32,128]{2,1,0:T(8,128)(4,1)S(1)} %get-tuple-element.15, pred[16,32,128]{2,1,0:T(8,128)(4,1)S(1)} %get-tuple-element.14, pred[16,32,128]{2,1,0:T(8,128)(4,1)S(1)} %get-tuple-element.13, ...), kind=kLoop, calls=%fused_computation.235 | loop fusion | flops 786432 | bytes 1048624 | tf_op jit(solution)/shard_map/stack | solution.py:229
  115.3 2.9 collective-permute-start
  118.2 2.6 collective-permute-start.1
  127.4 3.1 reduce
  130.6 4.9 %reshape.1300 = f32[2048,2,1,2,32]{4,3,2,1,0:T(2,128)} reshape(f32[16,16384]{1,0:T(8,128)S(1)} %reduce) | data formatting | bytes 2097152
  135.5 5.2 %copy.454 = f32[2,2,1,32,16,128]{5,3,4,1,2,0:T(8,128)S(1)} copy(f32[2,2,1,32,16,128]{3,1,0,5,4,2:T(2,128)} %bitcast.734) | data formatting | bytes 2097152 | tf_op jit(solution)/shard_map/all_to_all | solution.py:155
  157.3 6.7 %all-to-all-start.3 = ((f32[16,2,2,1,32,128]{5,4,2,3,1,0:T(8,128)}), f32[16,2,2,1,32,128]{5,4,2,3,1,0:T(8,128)S(1)}, u32[]{:S(2)}, u32[]{:S(2)}) async-start(f32[16,2,2,1,32,128]{5,4,2,3,1,0:T(8,128)} %bitcast.150), calls=%async_computation.3 | async-start | bytes 2097152 | tf_op jit(solution)/shard_map/all_to_all | solution.py:15
  169.6 9.7 %collective-permute-done.2 = f32[2,16,16,128]{3,2,1,0:T(8,128)S(1)} collective-permute-done((f32[2,16,16,128]{3,2,1,0:T(8,128)S(1)}, f32[2,16,16,128]{3,2,1,0:T(8,128)S(1)}, u32[]{:S(2)}, u32[]{:S(2)}) %collective-permute-start.2) | collective-permute-done | bytes 262176 | tf_op jit(solution)/shard_map/ppermute | solution.py:26
  189.1 20.6 %all_to_all.88 = f32[2,2,16,32,128]{4,3,1,0,2:T(8,128)S(1)} all-to-all(f32[2,2,16,32,128]{4,3,1,0,2:T(8,128)S(1)} %copy.486), channel_id=1, replica_groups=mesh['row'=16,'col'=16] {'row'}, dimensions={2} | all-to-all | bytes 2097152 | tf_op jit(solution)/shard_map/all_to_all | solution.py:143
  218.6 7.8 %all-to-all-start.5 = ((f32[2,2,1,512,128]{4,1,2,0,3:T(2,128)}), f32[2,2,1,512,128]{4,1,2,0,3:T(2,128)S(1)}, u32[]{:S(2)}, u32[]{:S(2)}) async-start(f32[2,2,1,512,128]{4,1,2,0,3:T(2,128)} %pad_maximum_fusion.3), calls=%async_computation.5 | async-start | bytes 2097152 | tf_op jit(solution)/shard_map/all_to_all | solution.py:146
  226.4 25.7 %all-to-all-done.5 = f32[2,2,1,512,128]{4,1,2,0,3:T(2,128)S(1)} async-done(((f32[2,2,1,512,128]{4,1,2,0,3:T(2,128)}), f32[2,2,1,512,128]{4,1,2,0,3:T(2,128)S(1)}, u32[]{:S(2)}, u32[]{:S(2)}) %all-to-all-start.5) | async-done | bytes 1048608 | tf_op jit(solution)/shard_map/all_to_all | solution.py:146
  274.5 24.4 %all_to_all.89 = f32[16,1,8192]{2,1,0:T(1,128)S(1)} all-to-all(f32[16,1,8192]{2,1,0:T(1,128)S(1)} %reshape.1301), channel_id=1, replica_groups=mesh['row'=16,'col'=16] {'col'}, dimensions={0} | all-to-all | bytes 1048576 | tf_op jit(solution)/shard_map/all_to_all | solution.py:155
  317.4 6.1 %all-to-all-start.7 = ((f32[16,2,1,1,32,128]{5,4,3,2,1,0:T(8,128)}), f32[16,2,1,1,32,128]{5,4,3,2,1,0:T(8,128)S(1)}, u32[]{:S(2)}, u32[]{:S(2)}) async-start(f32[16,2,1,1,32,128]{5,4,3,2,1,0:T(8,128)} %bitcast.258), calls=%async_computation.7 | async-start | bytes 1048576 | tf_op jit(solution)/shard_map/all_to_all | solution.py:15
  323.6 9.7 %all-to-all-done.7 = f32[16,2,1,1,32,128]{5,4,3,2,1,0:T(8,128)S(1)} async-done(((f32[16,2,1,1,32,128]{5,4,3,2,1,0:T(8,128)}), f32[16,2,1,1,32,128]{5,4,3,2,1,0:T(8,128)S(1)}, u32[]{:S(2)}, u32[]{:S(2)}) %all-to-all-start.7) | async-done | bytes 524320 | tf_op jit(solution)/shard_map/all_to_all | solution.py:15
  (233 shorter events, 117.5 us)
Async XLA Ops:
  5.2 16.6 %all-to-all-start = ((f32[2,1,16,32,128]{4,3,1,0,2:T(8,128)}), f32[2,1,16,32,128]{4,3,1,0,2:T(8,128)S(1)}, u32[]{:S(2)}, u32[]{:S(2)}) async-start(f32[2,1,16,32,128]{4,3,1,0,2:T(8,128)} %copy.440), calls=%async_computation | async-start | bytes 1048576 | tf_op jit(solution)/shard_map/all_to_all | solution.py:143
  27.2 27.3 %all-to-all-start.1 = ((f32[2,1,1,512,128]{4,2,1,0,3:T(1,128)}), f32[2,1,1,512,128]{4,2,1,0,3:T(1,128)S(1)}, u32[]{:S(2)}, u32[]{:S(2)}) async-start(f32[2,1,1,512,128]{4,2,1,0,3:T(1,128)} %pad_maximum_fusion.7), calls=%async_computation.1 | async-start | bytes 1048576 | tf_op jit(solution)/shard_map/all_to_all | solution.py:146
  38.0 21.9 %copy-start.17 = (f32[32]{0:T(128)}, f32[32]{0:T(128)S(1)}, u32[]{:S(2)}) copy-start(f32[32]{0:T(128)S(1)} %get-tuple-element.78) | copy-start | bytes 388
  38.6 21.3 %copy-start.20 = (f32[32]{0:T(128)}, f32[32]{0:T(128)S(1)}, u32[]{:S(2)}) copy-start(f32[32]{0:T(128)S(1)} %get-tuple-element.81) | copy-start | bytes 388
  76.6 4.1 %copy-start = (f32[2,1,32,32,64]{2,0,4,3,1:T(2,128)S(1)}, f32[2,1,32,32,64]{2,0,4,3,1:T(2,128)}, u32[]{:S(2)}) copy-start(f32[2,1,32,32,64]{2,0,4,3,1:T(2,128)} %copy.536) | copy-start | bytes 1572868
  85.9 11.1 %copy-start.22 = (f32[12]{0:T(128)S(1)}, f32[12]{0:T(128)}, u32[]{:S(2)}) copy-start(f32[12]{0:T(128)} %param.14) | copy-start | bytes 148
  85.9 11.1 %copy-start.23 = (f32[12]{0:T(128)S(1)}, f32[12]{0:T(128)}, u32[]{:S(2)}) copy-start(f32[12]{0:T(128)} %param.15) | copy-start | bytes 148
  85.9 12.6 %copy-start.7 = (s32[16,32,128]{2,1,0:T(8,128)S(1)}, s32[16,32,128]{2,1,0:T(8,128)}, u32[]{:S(2)}) copy-start(s32[16,32,128]{2,1,0:T(8,128)} %param.9) | copy-start | bytes 786436
  92.5 28.3 %copy-start.11 = (s32[4]{0:T(128)S(1)}, s32[4]{0:T(128)}, u32[]{:S(2)}) copy-start(s32[4]{0:T(128)} %param.17) | copy-start | bytes 52
  92.5 34.1 %copy-start.16 = (f32[33]{0:T(128)S(1)}, f32[33]{0:T(128)}, u32[]{:S(2)}) copy-start(f32[33]{0:T(128)} %param.16) | copy-start | bytes 400
  92.5 34.4 %all-to-all-start.2 = ((f32[16,1,16384]{2,1,0:T(1,128)}), f32[16,1,16384]{2,1,0:T(1,128)S(1)}, u32[]{:S(2)}, u32[]{:S(2)}) async-start(f32[16,1,16384]{2,1,0:T(1,128)} %reshape.1299), calls=%async_computation.2 | async-start | bytes 2097152 | tf_op jit(solution)/shard_map/all_to_all | solution.py:155
  115.3 48.7 %collective-permute-start = (f32[2,16,32,16]{3,2,1,0:T(8,128)}, f32[2,16,32,16]{3,2,1,0:T(8,128)}, u32[]{:S(2)}, u32[]{:S(2)}) collective-permute-start(f32[2,16,32,16]{3,2,1,0:T(8,128)} %get-tuple-element.44), channel_id=1, source_target_pairs={{0,1},{1,2},{2,3},{3,4},{4,5},{5,6},{6,7},{7,8},{8,9},{9,10},{10,1... | collective-permute-start | bytes 196616 | tf_op jit(solution)/shard_map/ppermute | solution.py:26
  118.2 45.9 %collective-permute-start.1 = (f32[2,16,32,16]{3,2,1,0:T(8,128)S(1)}, f32[2,16,32,16]{3,2,1,0:T(8,128)}, u32[]{:S(2)}, u32[]{:S(2)}) collective-permute-start(f32[2,16,32,16]{3,2,1,0:T(8,128)S(1)} %get-tuple-element.45), channel_id=1, source_target_pairs={{1,0},{2,1},{3,2},{4,3},{5,4},{6,5},{7,6},{8,7},{9,8},{10,9},{11,1... | collective-permute-start | bytes 196616 | tf_op jit(solution)/shard_map/ppermute | solution.py:27
  157.3 24.2 %all-to-all-start.3 = ((f32[16,2,2,1,32,128]{5,4,2,3,1,0:T(8,128)}), f32[16,2,2,1,32,128]{5,4,2,3,1,0:T(8,128)S(1)}, u32[]{:S(2)}, u32[]{:S(2)}) async-start(f32[16,2,2,1,32,128]{5,4,2,3,1,0:T(8,128)} %bitcast.150), calls=%async_computation.3 | async-start | bytes 2097152 | tf_op jit(solution)/shard_map/all_to_all | solution.py:15
  166.5 12.8 %collective-permute-start.2 = (f32[2,16,16,128]{3,2,1,0:T(8,128)S(1)}, f32[2,16,16,128]{3,2,1,0:T(8,128)S(1)}, u32[]{:S(2)}, u32[]{:S(2)}) collective-permute-start(f32[2,16,16,128]{3,2,1,0:T(8,128)S(1)} %get-tuple-element.42), channel_id=1, source_target_pairs={{0,16},{16,32},{32,48},{48,64},{64,80},{80,96},{96,112},{112,128},... | collective-permute-start | bytes 786440 | tf_op jit(solution)/shard_map/ppermute | solution.py:26
  168.2 12.6 %collective-permute-start.3 = (f32[2,16,16,128]{3,2,1,0:T(8,128)S(1)}, f32[2,16,16,128]{3,2,1,0:T(8,128)S(1)}, u32[]{:S(2)}, u32[]{:S(2)}) collective-permute-start(f32[2,16,16,128]{3,2,1,0:T(8,128)S(1)} %get-tuple-element.43), channel_id=1, source_target_pairs={{16,0},{32,16},{48,32},{64,48},{80,64},{96,80},{112,96},{128,112},... | collective-permute-start | bytes 786440 | tf_op jit(solution)/shard_map/ppermute | solution.py:27
  181.5 3.8 %copy-start.2 = (f32[2,16,32,128]{3,2,1,0:T(8,128)}, f32[2,16,32,128]{3,2,1,0:T(8,128)S(1)}, u32[]{:S(2)}) copy-start(f32[2,16,32,128]{3,2,1,0:T(8,128)S(1)} %convolution_bitcast_fusion) | copy-start | bytes 1572868
  185.6 3.0 copy-start.4
  218.6 33.4 %all-to-all-start.5 = ((f32[2,2,1,512,128]{4,1,2,0,3:T(2,128)}), f32[2,2,1,512,128]{4,1,2,0,3:T(2,128)S(1)}, u32[]{:S(2)}, u32[]{:S(2)}) async-start(f32[2,2,1,512,128]{4,1,2,0,3:T(2,128)} %pad_maximum_fusion.3), calls=%async_computation.5 | async-start | bytes 2097152 | tf_op jit(solution)/shard_map/all_to_all | solution.py:146
  306.9 16.6 %copy-start.13 = (f32[32]{0:T(128)S(1)}, f32[32]{0:T(128)}, u32[]{:S(2)}) copy-start(f32[32]{0:T(128)} %multiply_exponential_fusion) | copy-start | bytes 388
  306.9 16.6 %copy-start.15 = (f32[128]{0:T(128)S(1)}, f32[128]{0:T(128)}, u32[]{:S(2)}) copy-start(f32[128]{0:T(128)} %multiply_exponential_fusion.1) | copy-start | bytes 1540
  307.6 26.8 %copy-start.1 = (f32[16,32,128]{2,1,0:T(8,128)S(1)}, f32[16,32,128]{2,1,0:T(8,128)}, u32[]{:S(2)}) copy-start(f32[16,32,128]{2,1,0:T(8,128)} %param.10) | copy-start | bytes 786436
  307.7 26.8 %copy-start.3 = (f32[2,16,32,128]{3,2,1,0:T(8,128)S(1)}, f32[2,16,32,128]{3,2,1,0:T(8,128)}, u32[]{:S(2)}) copy-start(f32[2,16,32,128]{3,2,1,0:T(8,128)} %copy-done.2) | copy-start | bytes 1572868
  317.4 15.9 %all-to-all-start.7 = ((f32[16,2,1,1,32,128]{5,4,3,2,1,0:T(8,128)}), f32[16,2,1,1,32,128]{5,4,3,2,1,0:T(8,128)S(1)}, u32[]{:S(2)}, u32[]{:S(2)}) async-start(f32[16,2,1,1,32,128]{5,4,3,2,1,0:T(8,128)} %bitcast.258), calls=%async_computation.7 | async-start | bytes 1048576 | tf_op jit(solution)/shard_map/all_to_all | solution.py:15
  (10 other events, 19.4 us)
